TPU v7x, 32 devices: a whole 2x2x4 slice. The times are simulated.
32 devices in a mesh: groups: 2 (over y), rows: 4 (over z), cols: 4 (over x, core), depth: 1.
Axes of the slice: x: 2, y: 2, z: 4, core: 2. Of those that a mesh axis runs over, the one named last changes fastest.
Arguments:
- tensor: float32 [128, 64, 128], P(('groups', 'rows'), 'cols', 'depth'), parts along dimension 0, may hold values from -6 to 6
- start_one: float32 [128, 64], P(('groups', 'rows')), parts along dimension 0, may hold values from -0.75 to 0.75
- start_two: float32 [128, 64], P(('groups', 'cols')), parts along dimension 0, may hold values from -0.75 to 0.75
- start_three: float32 [256, 32], P(('groups', 'depth')), parts along dimension 0, may hold values from -0.5 to 0.5
Outputs:
- final_one: float32 [128, 64], P(('groups', 'rows')), parts along dimension 0
- final_two: float32 [128, 64], P(('groups', 'cols')), parts along dimension 0
- final_three: float32 [256, 32], P(('groups', 'depth')), parts along dimension 0
- core_tensor: float32 [128, 64, 32], P('groups'), parts along dimension 0
There are 2 independent parts, one for each index of `groups`. A program takes and returns all parts, laid end to end along the dimension named above; each array names one. Nothing has to cross between parts.
All inputs are finite; a program needn't handle non-finite values.
Results may differ from a plain program's by a relative error of at most 0.0001.
Values sent between devices are 32-bit elements; how exact they have to be, the bound alone decides.
A program may use at most 64 MiB of HBM per device.

v0:
```python
import functools
import math

import jax
import jax.numpy as jnp
from jax import lax
from jax.experimental import pallas as pl
from jax.experimental.pallas import tpu as pltpu
from jax.sharding import PartitionSpec as P

NEWTON = 3


exact_mode = lax.Precision.HIGHEST


def newton_steps(matrix, reduce_gram):
    gram_matrix = reduce_gram(jnp.dot(matrix.T, matrix, precision=exact_mode))
    total = jnp.trace(gram_matrix) + 1e-06
    current = matrix / jnp.sqrt(total)
    gram_matrix = gram_matrix / total
    identity = jnp.eye(matrix.shape[1], dtype=jnp.float32)
    for newton_index in range(NEWTON):
        if newton_index > 0:
            gram_matrix = reduce_gram(jnp.dot(current.T, current, precision=exact_mode))
        current = jnp.dot(current, 1.5 * identity - 0.5 * gram_matrix, precision=exact_mode)
    return current


def general_body(tensor, start_one, start_two, start_three):
    first, second, third = (start_one, start_two, start_three)
    block_one, block_two, block_three = tensor.shape
    rank_one = first.shape[1]
    rank_two = second.shape[1]
    rank_three = third.shape[1]
    core_flat = None
    sectioned = jnp.einsum("ijk,jb->bik", tensor, second, precision=exact_mode)
    unfolded = jnp.einsum("bik,kc->ibc", sectioned, third, precision=exact_mode).reshape(
        block_one, rank_two * rank_three
    )
    share = lax.psum_scatter(unfolded, ("cols", "depth"), scatter_dimension=1, tiled=True)
    piece = lax.psum(jnp.dot(first.T, share, precision=exact_mode), "rows")
    z_part = jnp.dot(share, piece.T, precision=exact_mode)
    z_rows = lax.psum(z_part, ("cols", "depth"))
    first = newton_steps(z_rows, lambda matrix: lax.psum(matrix, "rows"))
    sectioned = jnp.einsum("ijk,ia->ajk", tensor, first, precision=exact_mode)
    unfolded = jnp.einsum("ajk,kc->jac", sectioned, third, precision=exact_mode).reshape(
        block_two, rank_one * rank_three
    )
    share = lax.psum_scatter(unfolded, ("rows", "depth"), scatter_dimension=1, tiled=True)
    piece = lax.psum(jnp.dot(second.T, share, precision=exact_mode), "cols")
    z_part = jnp.dot(share, piece.T, precision=exact_mode)
    z_rows = lax.psum(z_part, ("rows", "depth"))
    second = newton_steps(z_rows, lambda matrix: lax.psum(matrix, "cols"))
    unfolded = jnp.einsum("ajk,jb->kab", sectioned, second, precision=exact_mode).reshape(
        block_three, rank_one * rank_two
    )
    core_flat = lax.psum(
        jnp.dot(third.T, unfolded, precision=exact_mode), ("rows", "cols", "depth")
    )
    z_rows = lax.psum(jnp.dot(unfolded, core_flat.T, precision=exact_mode), ("rows", "cols"))
    third = newton_steps(z_rows, lambda matrix: lax.psum(matrix, "depth"))
    core_tensor = core_flat.reshape(rank_three, rank_one, rank_two).transpose(1, 2, 0)
    length_one = block_one * lax.axis_size("rows")
    length_two = block_two * lax.axis_size("cols")
    length_three = block_three * lax.axis_size("depth")
    return (
        first * math.sqrt(length_one),
        second * math.sqrt(length_two),
        third * math.sqrt(length_three),
        core_tensor,
    )


LANES = 128
SUBLANES = 8
VMEM_GRANT = 24 * 1024 * 1024
MESH = pl.DeviceIdType.MESH


def split(x):
    high = x.astype(jnp.bfloat16)
    low = (x - high.astype(jnp.float32)).astype(jnp.bfloat16)
    return high, low


def raw(a, b, dims=((1,), (0,))):
    return lax.dot_general(a, b, (dims, ((), ())), preferred_element_type=jnp.float32)


def mm(a, b, dims=((1,), (0,))):
    ah, al = split(a)
    bh, bl = split(b)
    return raw(ah, bh, dims) + (raw(al, bh, dims) + raw(ah, bl, dims))


def eye(n):
    return (lax.broadcasted_iota(jnp.int32, (n, n), 0) == lax.broadcasted_iota(jnp.int32, (n, n), 1)).astype(jnp.float32)


def newton_factor(z, gram):
    identity = eye(gram.shape[0])
    total = jnp.sum(z * z, axis=(0, 1), keepdims=True) + 1e-06
    gram = gram / total
    scale = 1.0 / jnp.sqrt(total)
    factor = 1.5 * identity - 0.5 * gram
    for _ in range(NEWTON - 1):
        square = mm(gram, gram)
        gram = mm(gram, 2.25 * identity - 1.5 * gram + 0.25 * square)
        factor = mm(factor, 1.5 * identity - 0.5 * gram)
    return factor * scale


def orth(z):
    return mm(z, newton_factor(z, mm(z, z, ((0,), (0,)))))


def turn(x, width):
    row = lax.broadcasted_iota(jnp.int32, x.shape, 1)
    group = lax.broadcasted_iota(jnp.int32, x.shape, 2) // width
    result = x
    for d in range(1, SUBLANES):
        moved = pltpu.roll(pltpu.roll(x, SUBLANES - d, 1), d * width, 2)
        result = jnp.where((group - row + SUBLANES) % SUBLANES == d, moved, result)
    return result


def pair_gram(cat):
    n = cat.shape[0]
    high, low = split(cat)
    both = jnp.concatenate([high, low], axis=0)
    prod = raw(both, both, ((1,), (1,)))
    return prod[:n, :n] + (prod[n:, :n] + prod[:n, n:])


def kernel(n_r, n_c, t_hbm, u1_hbm, u2_hbm, u3_hbm, o1_ref, o2_ref, o3_ref, core_ref,
           t_ref, u1_ref, u2_ref, u3_ref, load_sem, mine, abuf, u1buf, u2buf, kron, at, work, tbuf, zmid, zrow,
           a_send, a_recv, f_send, f_recv, u1_send, u1_recv, u2_send, u2_recv,
           t_send, t_recv, tf_send, tf_recv, zr_send, zr_recv):
    g = lax.axis_index("groups")
    r = lax.axis_index("rows")
    cl = lax.axis_index("cols")
    bi, bj, bk = t_ref.shape
    r1, r2, r3 = u1_ref.shape[1], u2_ref.shape[1], u3_ref.shape[0]
    lo = LANES // bj
    hi = r3 // lo
    n_x = n_c // 2
    d1, d2 = n_r * bi, n_c * bj
    ihi = bi // SUBLANES

    def device(rr, cc):
        return (g, rr, cc, 0)

    def col(dx, parity):
        return lax.rem(cl // 2 + dx, n_x) * 2 + parity

    def row(dr):
        return lax.rem(r + dr, n_r)

    own, other = lax.rem(cl, 2), 1 - lax.rem(cl, 2)

    barrier = pltpu.get_barrier_semaphore()
    for dr in range(n_r):
        for dc in range(n_c):
            if dr or dc:
                pl.semaphore_signal(barrier, inc=1, device_id=device(row(dr), lax.rem(cl + dc, n_c)), device_id_type=MESH)

    loads = [
        pltpu.make_async_copy(src, dst, load_sem.at[n])
        for n, (src, dst) in enumerate((
            (t_hbm, t_ref), (u3_hbm, u3_ref), (u2_hbm, u2_ref), (u1_hbm, u1_ref),
            (u2_hbm, u2buf.at[cl]), (u1_hbm, u1buf.at[r]), (t_hbm, tbuf.at[cl])))
    ]
    for load in loads:
        load.start()
    for load in loads:
        load.wait()
    t2 = t_ref[...].reshape(bi * bj, bk)
    x = mm(u3_ref[...], t2, ((1,), (1,)))
    tiles = jnp.stack([x[h * lo:(h + 1) * lo, q * LANES:(q + 1) * LANES] for h in range(hi) for q in range(ihi)])
    turned = turn(tiles, bj).reshape(hi, bi, LANES)
    mine[...] = turned
    abuf[cl, :, pl.ds(pl.multiple_of(r * bi, bi), bi), :] = turned

    pl.semaphore_wait(barrier, n_r * n_c - 1)

    def slot(rr, cc):
        return abuf.at[cc, :, pl.ds(pl.multiple_of(rr * bi, bi), bi), :]

    sends = []

    def push(src, dst, s_sem, r_sem, dev):
        copy = pltpu.make_async_remote_copy(src_ref=src, dst_ref=dst, send_sem=s_sem, recv_sem=r_sem, device_id=dev, device_id_type=MESH)
        copy.start()
        sends.append(copy)

    def await_in(dst, s_sem, r_sem, dev):
        pltpu.make_async_remote_copy(src_ref=dst, dst_ref=dst, send_sem=s_sem, recv_sem=r_sem, device_id=dev, device_id_type=MESH).wait_recv()

    for dc in range(1, n_c):
        push(u2_ref, u2buf.at[cl], u2_send.at[dc], u2_recv.at[dc], device(r, lax.rem(cl + dc, n_c)))
    order = [(dr, dx) for dr in range(n_r) for dx in range(n_x) if dr or dx]
    for dr, dx in order:
        n = dr * n_x + dx
        push(mine, slot(r, cl), a_send.at[n], a_recv.at[n], device(row(dr), col(dx, own)))
    push(mine, slot(r, cl), f_send.at[0], f_recv.at[0], device(r, col(0, other)))
    for dr in range(1, n_r):
        push(u1_ref, u1buf.at[r], u1_send.at[dr], u1_recv.at[dr], device(row(dr), cl))

    for dx in range(1, n_x):
        push(t_ref, tbuf.at[cl], t_send.at[dx], t_recv.at[dx], device(r, col(dx, own)))
    push(t_ref, tbuf.at[cl], tf_send.at[0], tf_recv.at[0], device(r, col(0, other)))

    for dc in range(1, n_c):
        src = lax.rem(cl + n_c - dc, n_c)
        await_in(u2buf.at[src], u2_send.at[dc], u2_recv.at[dc], device(r, src))
    mask = (lax.broadcasted_iota(jnp.int32, (LANES, lo * r2), 0) // bj) == (lax.broadcasted_iota(jnp.int32, (LANES, lo * r2), 1) // r2)
    for c in range(n_c):
        block = jnp.concatenate([u2buf[c]] * lo, axis=0)
        block = jnp.concatenate([block, block], axis=1)
        block = jnp.where(mask, jnp.concatenate([block] * (lo // 2), axis=1), 0.0)
        kh, kl = split(block)
        kron[0, c * LANES:(c + 1) * LANES, :] = kh
        kron[1, c * LANES:(c + 1) * LANES, :] = kl

    for dr, dx in order:
        n = dr * n_x + dx
        rr, cc = lax.rem(r + n_r - dr, n_r), lax.rem(cl // 2 + n_x - dx, n_x) * 2 + own
        await_in(slot(rr, cc), a_send.at[n], a_recv.at[n], device(rr, cc))
        push(slot(rr, cc), slot(rr, cc), f_send.at[n], f_recv.at[n], device(r, col(0, other)))
    for dr, dx in [(0, 0)] + order:
        n = dr * n_x + dx
        rr, cc = lax.rem(r + n_r - dr, n_r), lax.rem(cl // 2 + n_x - dx, n_x) * 2 + other
        await_in(slot(rr, cc), f_send.at[n], f_recv.at[n], device(r, col(0, other)))
    for dr in range(1, n_r):
        src = lax.rem(r + n_r - dr, n_r)
        await_in(u1buf.at[src], u1_send.at[dr], u1_recv.at[dr], device(src, cl))

    block = jnp.concatenate([abuf[c].reshape(hi * d1, LANES) for c in range(n_c)], axis=1)
    bh, bl = split(block)
    kh = kron[0]
    y1 = raw(bh, kh) + (raw(bl, kh) + raw(bh, kron[1]))
    m1 = pair_gram(jnp.concatenate([y1[h * d1:(h + 1) * d1] for h in range(hi)], axis=1))
    bhf, blf = bh.astype(jnp.float32), bl.astype(jnp.float32)
    for h in range(hi):
        part = jnp.concatenate([bhf[h * d1:(h + 1) * d1], blf[h * d1:(h + 1) * d1]], axis=0)
        at[h] = part.T.astype(jnp.bfloat16)
    first = orth(mm(m1, u1buf[...].reshape(d1, r1)))
    work[0] = first
    first_own = work[0, pl.ds(pl.multiple_of(r * bi, bi), bi), :]
    o1_ref[...] = first_own * math.sqrt(d1)

    for dx in range(1, n_x):
        cc = lax.rem(cl // 2 + n_x - dx, n_x) * 2 + own
        await_in(tbuf.at[cc], t_send.at[dx], t_recv.at[dx], device(r, cc))
        push(tbuf.at[cc], tbuf.at[cc], tf_send.at[dx], tf_recv.at[dx], device(r, col(0, other)))

    fh, fl = split(first)
    zero = jnp.zeros_like(fh)
    rhs = jnp.concatenate([
        jnp.concatenate([fh, zero, fl, zero], axis=1),
        jnp.concatenate([fh, zero, zero, zero], axis=1),
        jnp.concatenate([zero, fh, zero, fl], axis=1),
        jnp.concatenate([zero, fh, zero, zero], axis=1)], axis=0)
    pieces = []
    for h in range(hi):
        even = jnp.concatenate([at[h, (q * lo + s) * bj:(q * lo + s + 1) * bj, :] for s in range(0, lo, 2) for q in range(n_c)], axis=0)
        odd = jnp.concatenate([at[h, (q * lo + s) * bj:(q * lo + s + 1) * bj, :] for s in range(1, lo, 2) for q in range(n_c)], axis=0)
        prod = raw(jnp.concatenate([even, odd], axis=1), rhs)
        prod = prod[:, :2 * r1] + prod[:, 2 * r1:]
        pieces += [prod[s * d2:(s + 1) * d2] for s in range(lo // 2)]
    y2 = jnp.concatenate(pieces, axis=1)
    m2 = pair_gram(y2)
    second = orth(mm(m2, u2buf[...].reshape(d2, r2)))
    work[1] = second
    second_own = work[1, pl.ds(pl.multiple_of(cl * bj, bj), bj), :]
    o2_ref[...] = second_own * math.sqrt(d2)

    v = mm(mm(second, second, ((1,), (1,))), y2)
    v = jnp.concatenate([v[:, h * lo * r1:(h + 1) * lo * r1] for h in range(hi)], axis=0)
    spread = jnp.concatenate([first_own] * lo, axis=0)
    spread = jnp.concatenate([spread, spread], axis=1)
    spread = jnp.concatenate([spread] * (lo // 2), axis=1)
    mask3 = (lax.broadcasted_iota(jnp.int32, (LANES, lo * r1), 0) // bi) == (lax.broadcasted_iota(jnp.int32, (LANES, lo * r1), 1) // r1)
    spread = jnp.where(mask3, spread, 0.0)
    w = mm(v, spread, ((1,), (1,)))
    jhi = d2 // SUBLANES
    w = turn(w.reshape(hi * jhi, SUBLANES, LANES), bi)
    w = jnp.concatenate([jnp.concatenate([w[h * jhi + q] for q in range(jhi)], axis=1) for h in range(hi)], axis=0)
    for dx in range(n_x):
        cc = lax.rem(cl // 2 + n_x - dx, n_x) * 2 + other
        await_in(tbuf.at[cc], tf_send.at[dx], tf_recv.at[dx], device(r, col(0, other)))
    tperm = jnp.concatenate([tbuf[c, :, j, :] for c in range(n_c) for j in range(bj)], axis=0)
    z = mm(w, tperm)
    zmid[...] = z
    for dr in range(1, n_r):
        push(zmid, zrow.at[dr], zr_send.at[dr], zr_recv.at[dr], device(row(dr), cl))

    yh, yl = split(y2)
    both = jnp.concatenate([yh.astype(jnp.float32), yl.astype(jnp.float32)], axis=0)
    sh, sl = split(second)
    high = jnp.concatenate([sh, sh], axis=0)
    low = jnp.concatenate([sl, jnp.zeros_like(sl)], axis=0)
    lhs = both.T.astype(jnp.bfloat16)
    core = (raw(lhs, high) + raw(lhs, low)).reshape(r3, r1, r2)

    for c in range(r3):
        core_ref[:, c, :] = core[c]
    for dr in range(1, n_r):
        await_in(zrow.at[dr], zr_send.at[dr], zr_recv.at[dr], device(lax.rem(r + n_r - dr, n_r), cl))
        z = z + zrow[dr]
    o3_ref[...] = mm(newton_factor(z, mm(z, z, ((1,), (1,)))), z) * math.sqrt(bk)
    for copy in sends:
        copy.wait_send()


def finish(*refs):
    copies = [pltpu.make_async_copy(refs[n], refs[4 + n], refs[8].at[n]) for n in range(4)]
    for copy in copies:
        copy.start()
    for copy in copies:
        copy.wait()


def fused_body(tensor, start_one, start_two, start_three):
    n_r, n_c = lax.axis_size("rows"), lax.axis_size("cols")
    bi, bj, bk = tensor.shape
    r1, r2, r3 = start_one.shape[1], start_two.shape[1], start_three.shape[1]
    lo = LANES // bj
    hi = r3 // lo
    d1, d2 = n_r * bi, n_c * bj
    f32, bf16 = jnp.float32, jnp.bfloat16
    vmem = pl.BlockSpec(memory_space=pltpu.VMEM)
    anywhere = pl.BlockSpec(memory_space=pl.ANY)
    dma = pltpu.SemaphoreType.DMA
    n_a = n_r * n_c // 2
    final_one, final_two, final_three, core = pl.pallas_call(
        functools.partial(kernel, n_r, n_c),
        out_shape=(
            jax.ShapeDtypeStruct((bi, r1), f32),
            jax.ShapeDtypeStruct((bj, r2), f32),
            jax.ShapeDtypeStruct((r3, bk), f32),
            jax.ShapeDtypeStruct((r1, r3, r2), f32),
        ),
        in_specs=[pl.BlockSpec(memory_space=pltpu.HBM)] * 4,
        out_specs=[vmem] * 4,
        scratch_shapes=[
            pltpu.VMEM((bi, bj, bk), f32),
            pltpu.VMEM((bi, r1), f32),
            pltpu.VMEM((bj, r2), f32),
            pltpu.VMEM((r3, bk), f32),
            dma((7,)),
            pltpu.VMEM((hi, bi, LANES), f32),
            pltpu.VMEM((n_c, hi, d1, LANES), f32),
            pltpu.VMEM((n_r, bi, r1), f32),
            pltpu.VMEM((n_c, bj, r2), f32),
            pltpu.VMEM((2, n_c * LANES, lo * r2), bf16),
            pltpu.VMEM((hi, n_c * LANES, 2 * d1), bf16),
            pltpu.VMEM((2, max(d1, d2), max(r1, r2)), f32),
            pltpu.VMEM((n_c, bi, bj, bk), f32),
            pltpu.VMEM((r3, bk), f32),
            pltpu.VMEM((n_r, r3, bk), f32),
            dma((n_a,)), dma((n_a,)), dma((n_a,)), dma((n_a,)),
            dma((n_r,)), dma((n_r,)), dma((n_c,)), dma((n_c,)),
            dma((n_c // 2,)), dma((n_c // 2,)), dma((n_c // 2,)), dma((n_c // 2,)),
            dma((n_r,)), dma((n_r,)),
        ],
        compiler_params=pltpu.CompilerParams(collective_id=0, has_side_effects=True, vmem_limit_bytes=VMEM_GRANT),
    )(*(pltpu.with_memory_space_constraint(x, pltpu.HBM) for x in (tensor, start_one, start_two, start_three.T)))
    results = (final_one, final_two, final_three, core)
    final_one, final_two, final_three, core = pl.pallas_call(
        finish,
        out_shape=tuple(jax.ShapeDtypeStruct(x.shape, f32) for x in results),
        in_specs=[vmem] * 4,
        out_specs=[anywhere] * 4,
        scratch_shapes=[dma((4,))],
        compiler_params=pltpu.CompilerParams(vmem_limit_bytes=VMEM_GRANT),
    )(*results)
    return final_one, final_two, final_three.T, core.transpose(0, 2, 1)


def body(tensor, start_one, start_two, start_three):
    bi, bj, bk = tensor.shape
    r1, r2, r3 = start_one.shape[1], start_two.shape[1], start_three.shape[1]
    n_r, n_c = lax.axis_size("rows"), lax.axis_size("cols")
    fits = (
        lax.axis_size("depth") == 1
        and n_c % 2 == 0
        and bi * SUBLANES == LANES
        and bj * SUBLANES == LANES
        and r3 % SUBLANES == 0
        and 2 * r1 == LANES
        and 2 * r2 == LANES
        and 2 * n_r * bi == LANES
        and 2 * n_c * bj == LANES
        and bk % LANES == 0
    )
    return (fused_body if fits else general_body)(tensor, start_one, start_two, start_three)


def solution(mesh):
    in_specs = (
        P(("groups", "rows"), "cols", "depth"),
        P(("groups", "rows"), None),
        P(("groups", "cols"), None),
        P(("groups", "depth"), None),
    )
    out_specs = (
        P(("groups", "rows"), None),
        P(("groups", "cols"), None),
        P(("groups", "depth"), None),
        P("groups", None, None),
    )
    return jax.shard_map(body, mesh=mesh, in_specs=in_specs, out_specs=out_specs, check_vma=False)
```

profile of v0, /device:TPU:0, one launch (start us, length us, event | category | flops | bytes accessed | tf_op | source)
XLA Modules:
  0.0 27.4 jit_solution(15558779080194797880)
XLA Ops:
  0.6 25.8 %shard_map.75 = (f32[16,64]{1,0:T(8,128)S(1)}, f32[16,64]{1,0:T(8,128)S(1)}, f32[32,128]{1,0:T(8,128)S(1)}, f32[64,32,64]{2,1,0:T(8,128)S(1)}) custom-call(f32[16,16,128]{2,1,0:T(8,128)} %t_hbm.1, f32[16,64]{1,0:T(8,128)} %u1_hbm.1, f32[16,64]{1,0:T(8,128)} %u2_hbm.1, f32[32,128]{1,0:T(8,128)} %bitcast.3), custom_call_target="tpu_custom_call" | custom-call | tf_op jit(solution)/shard_map/pallas_call | solution.py:337
  26.4 1.0 %shard_map.76 = (f32[16,64]{1,0:T(8,128)}, f32[16,64]{1,0:T(8,128)}, f32[32,128]{1,0:T(8,128)}, f32[64,32,64]{2,1,0:T(8,128)}) custom-call(f32[16,64]{1,0:T(8,128)S(1)} %get-tuple-element.12.refs_0_, f32[16,64]{1,0:T(8,128)S(1)} %get-tuple-element.13.refs_1_, f32[32,128]{1,0:T(8,128)S(1)} %get-tuple-element.14.refs_2_, ...), custom_call_target="tpu_custom_call" | custom-call | tf_op jit(solution)/shard_map/pallas_call | solution.py:371
where the time goes:
time: 27.6 us; the launch traced here: 27.4 us
  Pallas kernels  26.8 us (97%)
  between operations  0.64 us (2%)
    pallas_call x1, Pallas kernels, fused_body(): pl.pallas_call(functools.partial(kernel, n_r, n_c), out_shape=(jax.ShapeD...  25.8 us
    pallas_call x1, Pallas kernels, fused_body(): pl.pallas_call(finish, out_shape=tuple((jax.ShapeDtypeStruct(x.shape, f32...  1.02 us

commit v1 on v0

--- a/solution.py
+++ b/solution.py
@@ -98,21 +98,48 @@
     return (lax.broadcasted_iota(jnp.int32, (n, n), 0) == lax.broadcasted_iota(jnp.int32, (n, n), 1)).astype(jnp.float32)
 
 
-def newton_factor(z, gram):
-    identity = eye(gram.shape[0])
+def products(lefts, b):
+    parts = [split(a) for a in lefts]
+    bh, bl = split(b)
+    top = raw(jnp.concatenate([p[0] for p in parts] + [p[1] for p in parts], axis=0), bh)
+    bottom = raw(jnp.concatenate([p[0] for p in parts], axis=0), bl)
+    half, results, at = bottom.shape[0], [], 0
+    for a in lefts:
+        n = a.shape[0]
+        results.append(top[at:at + n] + (top[half + at:half + at + n] + bottom[at:at + n]))
+        at += n
+    return results
+
+
+def normalized(z, gram):
     total = jnp.sum(z * z, axis=(0, 1), keepdims=True) + 1e-06
-    gram = gram / total
-    scale = 1.0 / jnp.sqrt(total)
-    factor = 1.5 * identity - 0.5 * gram
-    for _ in range(NEWTON - 1):
+    return gram * (1.0 / total), 1.0 / jnp.sqrt(total)
+
+
+def next_gram(gram, square):
+    return mm(gram, 2.25 * eye(gram.shape[0]) - 1.5 * gram + 0.25 * square)
+
+
+def orth(z, carried=None):
+    gram, scale = normalized(z, mm(z, z, ((0,), (0,))))
+    for n in range(NEWTON - 1):
+        step, square = products([z, gram], gram)
+        z = 1.5 * z - 0.5 * step
+        gram = next_gram(gram, square)
+    result = (1.5 * z - 0.5 * mm(z, gram)) * scale
+    if carried is None:
+        return result
+    inner = mm(z, carried, ((0,), (0,)))
+    return result, (1.5 * inner - 0.5 * mm(gram, inner)) * scale
+
+
+def orth_rows(z):
+    gram, scale = normalized(z, mm(z, z, ((1,), (1,))))
+    for n in range(NEWTON - 1):
         square = mm(gram, gram)
-        gram = mm(gram, 2.25 * identity - 1.5 * gram + 0.25 * square)
-        factor = mm(factor, 1.5 * identity - 0.5 * gram)
-    return factor * scale
-
-
-def orth(z):
-    return mm(z, newton_factor(z, mm(z, z, ((0,), (0,)))))
+        z = 1.5 * z - 0.5 * mm(gram, z)
+        gram = next_gram(gram, square)
+    return (1.5 * z - 0.5 * mm(gram, z)) * scale
 
 
 def turn(x, width):
@@ -133,8 +160,8 @@
     return prod[:n, :n] + (prod[n:, :n] + prod[:n, n:])
 
 
-def kernel(n_r, n_c, t_hbm, u1_hbm, u2_hbm, u3_hbm, o1_ref, o2_ref, o3_ref, core_ref,
-           t_ref, u1_ref, u2_ref, u3_ref, load_sem, mine, abuf, u1buf, u2buf, kron, at, work, tbuf, zmid, zrow,
+def kernel(n_r, n_c, t_hbm, u1_hbm, u2_hbm, u3_hbm, o1_ref, o2_ref, zsum_ref, core_ref,
+           t_ref, u1_ref, u2_ref, u3_ref, load_sem, mine, abuf, u1buf, u2buf, kron, at, work, tbuf, zrow,
            a_send, a_recv, f_send, f_recv, u1_send, u1_recv, u2_send, u2_recv,
            t_send, t_recv, tf_send, tf_recv, zr_send, zr_recv):
     g = lax.axis_index("groups")
@@ -157,13 +184,13 @@
     def row(dr):
         return lax.rem(r + dr, n_r)
 
+    def far_row(n):
+        up = r // (n_r // 2)
+        here = r + up * (n_r - 1 - 2 * r)
+        there = n_r - 1 - n - (here + n + 1) // n_r
+        return there + up * (n_r - 1 - 2 * there)
+
     own, other = lax.rem(cl, 2), 1 - lax.rem(cl, 2)
-
-    barrier = pltpu.get_barrier_semaphore()
-    for dr in range(n_r):
-        for dc in range(n_c):
-            if dr or dc:
-                pl.semaphore_signal(barrier, inc=1, device_id=device(row(dr), lax.rem(cl + dc, n_c)), device_id_type=MESH)
 
     loads = [
         pltpu.make_async_copy(src, dst, load_sem.at[n])
@@ -173,7 +200,14 @@
     ]
     for load in loads:
         load.start()
-    for load in loads:
+
+    barrier = pltpu.get_barrier_semaphore()
+    for dr in range(n_r):
+        for dc in range(n_c):
+            if dr or dc:
+                pl.semaphore_signal(barrier, inc=1, device_id=device(row(dr), lax.rem(cl + dc, n_c)), device_id_type=MESH)
+
+    for load in loads[:2]:
         load.wait()
     t2 = t_ref[...].reshape(bi * bj, bk)
     x = mm(u3_ref[...], t2, ((1,), (1,)))
@@ -182,6 +216,8 @@
     mine[...] = turned
     abuf[cl, :, pl.ds(pl.multiple_of(r * bi, bi), bi), :] = turned
 
+    for load in loads[2:]:
+        load.wait()
     pl.semaphore_wait(barrier, n_r * n_c - 1)
 
     def slot(rr, cc):
@@ -245,15 +281,15 @@
     for h in range(hi):
         part = jnp.concatenate([bhf[h * d1:(h + 1) * d1], blf[h * d1:(h + 1) * d1]], axis=0)
         at[h] = part.T.astype(jnp.bfloat16)
+    for dx in range(1, n_x):
+        cc = lax.rem(cl // 2 + n_x - dx, n_x) * 2 + own
+        await_in(tbuf.at[cc], t_send.at[dx], t_recv.at[dx], device(r, cc))
+        push(tbuf.at[cc], tbuf.at[cc], tf_send.at[dx], tf_recv.at[dx], device(r, col(0, other)))
+
     first = orth(mm(m1, u1buf[...].reshape(d1, r1)))
     work[0] = first
     first_own = work[0, pl.ds(pl.multiple_of(r * bi, bi), bi), :]
     o1_ref[...] = first_own * math.sqrt(d1)
-
-    for dx in range(1, n_x):
-        cc = lax.rem(cl // 2 + n_x - dx, n_x) * 2 + own
-        await_in(tbuf.at[cc], t_send.at[dx], t_recv.at[dx], device(r, cc))
-        push(tbuf.at[cc], tbuf.at[cc], tf_send.at[dx], tf_recv.at[dx], device(r, col(0, other)))
 
     fh, fl = split(first)
     zero = jnp.zeros_like(fh)
@@ -271,30 +307,35 @@
         pieces += [prod[s * d2:(s + 1) * d2] for s in range(lo // 2)]
     y2 = jnp.concatenate(pieces, axis=1)
     m2 = pair_gram(y2)
-    second = orth(mm(m2, u2buf[...].reshape(d2, r2)))
-    work[1] = second
-    second_own = work[1, pl.ds(pl.multiple_of(cl * bj, bj), bj), :]
-    o2_ref[...] = second_own * math.sqrt(d2)
-
-    v = mm(mm(second, second, ((1,), (1,))), y2)
-    v = jnp.concatenate([v[:, h * lo * r1:(h + 1) * lo * r1] for h in range(hi)], axis=0)
     spread = jnp.concatenate([first_own] * lo, axis=0)
     spread = jnp.concatenate([spread, spread], axis=1)
     spread = jnp.concatenate([spread] * (lo // 2), axis=1)
     mask3 = (lax.broadcasted_iota(jnp.int32, (LANES, lo * r1), 0) // bi) == (lax.broadcasted_iota(jnp.int32, (LANES, lo * r1), 1) // r1)
     spread = jnp.where(mask3, spread, 0.0)
-    w = mm(v, spread, ((1,), (1,)))
-    jhi = d2 // SUBLANES
-    w = turn(w.reshape(hi * jhi, SUBLANES, LANES), bi)
-    w = jnp.concatenate([jnp.concatenate([w[h * jhi + q] for q in range(jhi)], axis=1) for h in range(hi)], axis=0)
+    wide = jnp.concatenate([y2[:, h * lo * r1:(h + 1) * lo * r1] for h in range(hi)], axis=0)
+    wide = mm(wide, spread, ((1,), (1,)))
+    wide = jnp.concatenate([wide[h * d2:(h + 1) * d2] for h in range(hi)], axis=1)
     for dx in range(n_x):
         cc = lax.rem(cl // 2 + n_x - dx, n_x) * 2 + other
         await_in(tbuf.at[cc], tf_send.at[dx], tf_recv.at[dx], device(r, col(0, other)))
     tperm = jnp.concatenate([tbuf[c, :, j, :] for c in range(n_c) for j in range(bj)], axis=0)
-    z = mm(w, tperm)
-    zmid[...] = z
-    for dr in range(1, n_r):
-        push(zmid, zrow.at[dr], zr_send.at[dr], zr_recv.at[dr], device(row(dr), cl))
+    th, tl = split(tperm)
+    second, inner = orth(mm(m2, u2buf[...].reshape(d2, r2)), wide)
+    work[1] = second
+    second_own = work[1, pl.ds(pl.multiple_of(cl * bj, bj), bj), :]
+    o2_ref[...] = second_own * math.sqrt(d2)
+
+    w = mm(second, inner)
+    jhi = d2 // SUBLANES
+    w = jnp.concatenate([w[:, h * LANES:(h + 1) * LANES] for h in range(hi)], axis=0)
+    w = turn(w.reshape(hi * jhi, SUBLANES, LANES), bi)
+    w = jnp.concatenate([jnp.concatenate([w[h * jhi + q] for q in range(jhi)], axis=1) for h in range(hi)], axis=0)
+    wh, wl = split(w)
+    z = raw(jnp.concatenate([wh, wl], axis=0), th)
+    z = z[:r3] + (z[r3:] + raw(wh, tl))
+    zrow[r] = z
+    for n in range(n_r - 1):
+        push(zrow.at[r], zrow.at[r], zr_send.at[n], zr_recv.at[r], device(far_row(n), cl))
 
     yh, yl = split(y2)
     both = jnp.concatenate([yh.astype(jnp.float32), yl.astype(jnp.float32)], axis=0)
@@ -306,18 +347,23 @@
 
     for c in range(r3):
         core_ref[:, c, :] = core[c]
-    for dr in range(1, n_r):
-        await_in(zrow.at[dr], zr_send.at[dr], zr_recv.at[dr], device(lax.rem(r + n_r - dr, n_r), cl))
-        z = z + zrow[dr]
-    o3_ref[...] = mm(newton_factor(z, mm(z, z, ((1,), (1,)))), z) * math.sqrt(bk)
+    for n in reversed(range(n_r - 1)):
+        src = far_row(n)
+        await_in(zrow.at[src], zr_send.at[n], zr_recv.at[src], device(src, cl))
+    zsum_ref[...] = sum(zrow[n] for n in range(1, n_r)) + zrow[0]
     for copy in sends:
         copy.wait_send()
 
 
-def finish(*refs):
-    copies = [pltpu.make_async_copy(refs[n], refs[4 + n], refs[8].at[n]) for n in range(4)]
-    for copy in copies:
+def finish(o1_ref, o2_ref, zsum_ref, core_ref, o1_hbm, o2_hbm, o3_hbm, core_hbm, o3_ref, sem):
+    def out(n, src, dst):
+        copy = pltpu.make_async_copy(src, dst, sem.at[n])
         copy.start()
+        return copy
+
+    copies = [out(0, core_ref, core_hbm), out(1, o1_ref, o1_hbm), out(2, o2_ref, o2_hbm)]
+    o3_ref[...] = orth_rows(zsum_ref[...]) * math.sqrt(zsum_ref.shape[1])
+    copies.append(out(3, o3_ref, o3_hbm))
     for copy in copies:
         copy.wait()
 
@@ -358,7 +404,6 @@
             pltpu.VMEM((hi, n_c * LANES, 2 * d1), bf16),
             pltpu.VMEM((2, max(d1, d2), max(r1, r2)), f32),
             pltpu.VMEM((n_c, bi, bj, bk), f32),
-            pltpu.VMEM((r3, bk), f32),
             pltpu.VMEM((n_r, r3, bk), f32),
             dma((n_a,)), dma((n_a,)), dma((n_a,)), dma((n_a,)),
             dma((n_r,)), dma((n_r,)), dma((n_c,)), dma((n_c,)),
@@ -373,7 +418,7 @@
         out_shape=tuple(jax.ShapeDtypeStruct(x.shape, f32) for x in results),
         in_specs=[vmem] * 4,
         out_specs=[anywhere] * 4,
-        scratch_shapes=[dma((4,))],
+        scratch_shapes=[pltpu.VMEM((r3, bk), f32), dma((4,))],
         compiler_params=pltpu.CompilerParams(vmem_limit_bytes=VMEM_GRANT),
     )(*results)
     return final_one, final_two, final_three.T, core.transpose(0, 2, 1)

time: 27.6 us -> 25.9 us (0.938)
  Pallas kernels: 26.8 us -> 25.2 us
    pallas_call x1, Pallas kernels: 25.8 us -> 23.7 us  [fused_body(): pl.pallas_call(functools.partial(kernel, n_r, n_c), out_shape=(jax.ShapeD...]
    pallas_call x1, Pallas kernels: 1.02 us -> 1.46 us  [fused_body(): pl.pallas_call(finish, out_shape=tuple((jax.ShapeDtypeStruct(x.shape, f32...]
where the time goes in v1:
time: 25.9 us; the launch traced here: 25.8 us
  Pallas kernels  25.2 us (97%)
  between operations  0.64 us (2%)
    pallas_call x1, Pallas kernels, fused_body(): pl.pallas_call(functools.partial(kernel, n_r, n_c), out_shape=(jax.ShapeD...  23.7 us
    pallas_call x1, Pallas kernels, fused_body(): pl.pallas_call(finish, out_shape=tuple((jax.ShapeDtypeStruct(x.shape, f32...  1.46 us

profile of v1, /device:TPU:0, one launch (start us, length us, event | category | flops | bytes accessed | tf_op | source)
XLA Modules:
  0.0 25.8 jit_solution(7830345793662670683)
XLA Ops:
  0.6 23.7 %shard_map.75 = (f32[16,64]{1,0:T(8,128)S(1)}, f32[16,64]{1,0:T(8,128)S(1)}, f32[32,128]{1,0:T(8,128)S(1)}, f32[64,32,64]{2,1,0:T(8,128)S(1)}) custom-call(f32[16,16,128]{2,1,0:T(8,128)} %t_hbm.1, f32[16,64]{1,0:T(8,128)} %u1_hbm.1, f32[16,64]{1,0:T(8,128)} %u2_hbm.1, f32[32,128]{1,0:T(8,128)} %bitcast.3), custom_call_target="tpu_custom_call" | custom-call | tf_op jit(solution)/shard_map/pallas_call | solution.py:383
  24.3 1.5 %shard_map.76 = (f32[16,64]{1,0:T(8,128)}, f32[16,64]{1,0:T(8,128)}, f32[32,128]{1,0:T(8,128)}, f32[64,32,64]{2,1,0:T(8,128)}) custom-call(f32[16,64]{1,0:T(8,128)S(1)} %get-tuple-element.12.o1_ref, f32[16,64]{1,0:T(8,128)S(1)} %get-tuple-element.13.o2_ref, f32[32,128]{1,0:T(8,128)S(1)} %get-tuple-element.14.zsum_ref, ...), custom_call_target="tpu_custom_call" | custom-call | tf_op jit(solution)/shard_map/pallas_call | solution.py:416
